TPU v7x, 32 devices: a whole 2x2x4 slice. The times are simulated.
32 devices in a mesh: groups: 2 (over y), seq: 4 (over z), head: 2 (over x), inner: 2 (over core).
Axes of the slice: x: 2, y: 2, z: 4, core: 2. Of those that a mesh axis runs over, the one named last changes fastest.
Arguments:
- queries: bfloat16 [4096, 2, 8, 128], P(('groups', 'seq'), 'head', 'inner'), parts along dimension 0, may hold values from -120 to 120
- grad_out: bfloat16 [4096, 2, 8, 128], P(('groups', 'seq'), 'head', 'inner'), parts along dimension 0, may hold values from -6 to 6
- keys: bfloat16 [4096, 2, 128], P(('groups', 'seq'), 'head'), parts along dimension 0, may hold values from -6 to 6
- values: bfloat16 [4096, 2, 128], P(('groups', 'seq'), 'head'), parts along dimension 0, may hold values from -6 to 6
- indices: int32 [2, 64, 16], P('head', 'groups'), parts along dimension 1, may hold values from 0 to 31, as said below
- valid: int32 [2, 64, 16], P('head', 'groups'), parts along dimension 1, may hold values from 0 to 1
Outputs:
- grad_queries: bfloat16 [4096, 2, 8, 128], P(('groups', 'seq'), 'head', 'inner'), parts along dimension 0
- grad_keys: bfloat16 [4096, 2, 128], P(('groups', 'seq'), 'head'), parts along dimension 0
- grad_values: bfloat16 [4096, 2, 128], P(('groups', 'seq'), 'head'), parts along dimension 0
There are 2 independent parts, one for each index of `groups`. A program takes and returns all parts, laid end to end along the dimension named above; each array names one. Nothing has to cross between parts.
Inputs may be any that keep to these rules, and one draw needn't show every extreme that they name: `indices`: call blocks r * 8 to r * 8 + 7 run r. For every KV head and query block b: slot 0 names b and is valid; the valid slots name distinct blocks at most b; over all query blocks of run r, the valid slots name blocks of runs later than r never, and for each earlier run exactly 4 distinct blocks of it. Slots that are not valid name arbitrary blocks.
All inputs are finite; a program needn't handle non-finite values.
Results may differ from a plain program's by a relative error of at most 0.007.
Values may be sent and summed in bfloat16 or wider, within the bound.
No kernel may reach another device: no remote copies, remote signals or barrier semaphores. Data moves between devices by JAX's collectives and lax.ppermute only.
A program may use at most 64 MiB of HBM per device.

v0:
```python
import math
import jax
import jax.numpy as jnp
from jax import lax
from jax.sharding import PartitionSpec as P

BLK = 64
TOPK = 16
CAP = 4


def per_device(queries, grad_out, keys, values, indices, valid):
    tokens = queries.shape[0]
    heads_here = queries.shape[2]
    width = queries.shape[3]
    seq_count = lax.axis_size("seq")
    seq_here = lax.axis_index("seq")
    blocks_here = tokens // BLK
    total_blocks = indices.shape[1]
    scaling = 1.0 / math.sqrt(width)
    remote_rows = seq_count * CAP
    dest_rows = remote_rows + blocks_here
    picks_all = indices[0]
    valid_all = valid[0] > 0
    owner_all = picks_all // blocks_here
    local_all = picks_all % blocks_here
    my_picks = lax.dynamic_slice_in_dim(picks_all, seq_here * blocks_here, blocks_here, 0)
    my_valid = lax.dynamic_slice_in_dim(valid_all, seq_here * blocks_here, blocks_here, 0)
    my_owner = my_picks // blocks_here
    my_local = my_picks % blocks_here
    remote = my_valid & (my_owner != seq_here)
    block_ids = jnp.arange(total_blocks, dtype=jnp.int32)
    hits_in = (my_picks[:, :, None] == block_ids[None, None, :]) & remote[:, :, None]
    present_in = jnp.any(hits_in, axis=(0, 1)).reshape(seq_count, blocks_here)
    rank_in = jnp.cumsum(present_in.astype(jnp.int32), axis=1) - 1
    slot_ref = jnp.sum(jnp.where(hits_in, rank_in.reshape(-1)[None, None, :], 0), axis=2)
    row_index = jnp.where(remote, my_owner * CAP + slot_ref, remote_rows + my_local)
    source_run = block_ids // blocks_here
    incoming = valid_all & (owner_all == seq_here) & (source_run != seq_here)[:, None]
    hits_out = (
        local_all[:, :, None] == jnp.arange(blocks_here, dtype=jnp.int32)[None, None, :]
    ) & incoming[:, :, None]
    present_out = jnp.any(hits_out.reshape(seq_count, blocks_here * TOPK, blocks_here), axis=1)
    rank_out = jnp.cumsum(present_out.astype(jnp.int32), axis=1) - 1
    choose_out = present_out[:, None, :] & (
        rank_out[:, None, :] == jnp.arange(CAP, dtype=jnp.int32)[None, :, None]
    )
    wanted = my_picks.reshape(-1)
    blank = jnp.zeros((blocks_here * TOPK, BLK, width), jnp.bfloat16)
    carry = (blank, blank)
    key_piece = lax.all_gather(keys, "seq", axis=0, tiled=True)
    value_piece = lax.all_gather(values, "seq", axis=0, tiled=True)
    count = key_piece.shape[0] // BLK
    relative = wanted
    inside = (relative >= 0) & (relative < count)
    relative = jnp.clip(relative, 0, count - 1)
    key_rows = jnp.take(key_piece[:, 0].reshape(count, BLK, width), relative, axis=0)
    value_rows = jnp.take(value_piece[:, 0].reshape(count, BLK, width), relative, axis=0)
    sel_keys = jnp.where(inside[:, None, None], key_rows, carry[0])
    sel_values = jnp.where(inside[:, None, None], value_rows, carry[1])
    group = math.gcd(blocks_here, max(1, 512 // (BLK * heads_here)))
    steps_count = blocks_here // group
    span = TOPK * BLK
    position = jnp.arange(BLK, dtype=jnp.int32)
    causal = position[None, :] <= position[:, None]
    block_global = seq_here * blocks_here + jnp.arange(blocks_here, dtype=jnp.int32)
    before = my_picks < block_global[:, None]
    same = my_picks == block_global[:, None]
    allowed = my_valid[:, None, :, None] & (
        before[:, None, :, None] | same[:, None, :, None] & causal[None, :, None, :]
    )
    allowed = allowed.reshape(steps_count, group, BLK, span)
    query_steps = queries[:, 0].reshape(steps_count, group, BLK, heads_here, width)
    grad_steps = grad_out[:, 0].reshape(steps_count, group, BLK, heads_here, width)
    key_steps = sel_keys.reshape(steps_count, group, span, width)
    value_steps = sel_values.reshape(steps_count, group, span, width)
    row_steps = row_index.reshape(steps_count, group * TOPK)

    def attend(carry, inputs):
        key_acc, value_acc = carry
        q_group, do_group, k_group, v_group, mask_group, rows_group = inputs
        mask_heads = mask_group[:, None, :, :]
        scores = (
            jnp.einsum("qigw,qsw->qgis", q_group, k_group, preferred_element_type=jnp.float32)
            * scaling
        )
        highest = jnp.max(jnp.where(mask_heads, scores, -jnp.inf), axis=-1, keepdims=True)
        weights = jnp.where(mask_heads, jnp.exp(scores - highest), 0.0)
        probs = weights / jnp.sum(weights, axis=-1, keepdims=True)
        probs_b = probs.astype(jnp.bfloat16)
        dprobs = jnp.einsum("qigw,qsw->qgis", do_group, v_group, preferred_element_type=jnp.float32)
        delta = jnp.sum(probs * dprobs, axis=-1, keepdims=True)
        dscores = (probs * (dprobs - delta)).astype(jnp.bfloat16)
        query_grad = (
            jnp.einsum("qgis,qsw->qigw", dscores, k_group, preferred_element_type=jnp.float32)
            * scaling
        ).astype(jnp.bfloat16)
        key_terms = (
            jnp.einsum("qgis,qigw->qsw", dscores, q_group, preferred_element_type=jnp.float32)
            * scaling
        )
        value_terms = jnp.einsum(
            "qgis,qigw->qsw", probs_b, do_group, preferred_element_type=jnp.float32
        )
        key_acc = key_acc.at[rows_group].add(key_terms.reshape(group * TOPK, BLK * width))
        value_acc = value_acc.at[rows_group].add(value_terms.reshape(group * TOPK, BLK * width))
        return ((key_acc, value_acc), query_grad)

    zeros_dest = jnp.zeros((dest_rows, BLK * width), jnp.float32)
    (key_acc, value_acc), query_grads = lax.scan(
        attend,
        (zeros_dest, zeros_dest),
        (query_steps, grad_steps, key_steps, value_steps, allowed, row_steps),
    )
    grad_queries = query_grads.reshape(tokens, 1, heads_here, width)
    send_key_tiles = key_acc[:remote_rows].reshape(seq_count, CAP, BLK * width)
    send_value_tiles = value_acc[:remote_rows].reshape(seq_count, CAP, BLK * width)
    own_keys = key_acc[remote_rows:]
    own_values = value_acc[remote_rows:]
    choose_float = choose_out.astype(jnp.float32)
    back_keys, back_values = (
        lax.all_to_all(send_key_tiles, "seq", split_axis=0, concat_axis=0, tiled=True),
        lax.all_to_all(send_value_tiles, "seq", split_axis=0, concat_axis=0, tiled=True),
    )
    local_keys = own_keys + jnp.einsum(
        "dcb,dcx->bx", choose_float, back_keys, precision=lax.Precision.HIGHEST
    )
    local_values = own_values + jnp.einsum(
        "dcb,dcx->bx", choose_float, back_values, precision=lax.Precision.HIGHEST
    )
    total_keys, total_values = lax.psum((local_keys, local_values), "inner")
    grad_keys = total_keys.astype(jnp.bfloat16).reshape(tokens, 1, width)
    grad_values = total_values.astype(jnp.bfloat16).reshape(tokens, 1, width)
    return (grad_queries, grad_keys, grad_values)


def solution(mesh):
    return jax.shard_map(
        per_device,
        mesh=mesh,
        in_specs=(
            P(("groups", "seq"), "head", "inner", None),
            P(("groups", "seq"), "head", "inner", None),
            P(("groups", "seq"), "head", None),
            P(("groups", "seq"), "head", None),
            P("head", "groups", None),
            P("head", "groups", None),
        ),
        out_specs=(
            P(("groups", "seq"), "head", "inner", None),
            P(("groups", "seq"), "head", None),
            P(("groups", "seq"), "head", None),
        ),
        check_vma=False,
    )
```

profile of v0, /device:TPU:0, one launch (start us, length us, event | category | flops | bytes accessed | tf_op | source)
XLA Modules:
  0.0 166.9 jit_solution(11409170172867323838)
XLA Ops:
  4.3 17.6 %all_gather.6 = bf16[2048,1,128]{2,0,1:T(8,128)(2,1)S(1)} all-gather(bf16[512,1,128]{2,0,1:T(8,128)(2,1)} %param.12), channel_id=1, replica_groups=mesh['groups'=2,'seq'=4,'head'=2,'inner'=2] {'seq'}, dimensions={0}, use_global_device_ids=true | all-gather | bytes 655360 | tf_op jit(solution)/shard_map/all_gather | solution.py:51
  21.9 16.6 %all_gather.7 = bf16[2048,1,128]{2,0,1:T(8,128)(2,1)S(1)} all-gather(bf16[512,1,128]{2,0,1:T(8,128)(2,1)} %param.13), channel_id=1, replica_groups=mesh['groups'=2,'seq'=4,'head'=2,'inner'=2] {'seq'}, dimensions={0}, use_global_device_ids=true | all-gather | bytes 655360 | tf_op jit(solution)/shard_map/all_gather | solution.py:52
  39.4 2.1 %gather_fusion = bf16[128,64,128]{2,1,0:T(8,128)(2,1)} fusion(bf16[32,64,128]{2,1,0:T(8,128)(2,1)S(1)} %bitcast.131, s32[1024]{0:T(1024)S(1)} %pad_clamp_fusion), kind=kCustom, calls=%fused_computation.clone | custom fusion | bytes 4194816 | tf_op jit(solution)/shard_map/jit(_take)/gather | solution.py:57
  42.8 3.7 %select_select_fusion = (bf16[128,64,128]{2,1,0:T(8,128)(2,1)}, bf16[128,64,128]{2,1,0:T(8,128)(2,1)}) fusion(bf16[128,64,128]{2,1,0:T(8,128)(2,1)S(1)} %gather_fusion.1, pred[128]{0:T(512)(128)(4,1)S(1)} %compare_and_fusion.2, pred[128]{0:T(512)(128)(4,1)S(1)} %and.166, bf16[128,64,128]{2,1,0:T(8,128)(2,1)} %gather_fusion), kind=kLoop, calls=%fused_computation.54 | loop fusion | flops 4194304 | bytes 8388864 | tf_op jit(solution)/shard_map/jit(_where)/select_n | solution.py:60
  46.6 84.0 %while.14 = (s32[]{:T(128)}, f32[24,8192]{1,0:T(8,128)S(1)}, f32[24,8192]{1,0:T(8,128)S(1)}, bf16[4,2,64,4,128]{4,3,2,1,0:T(4,128)(2,1)}, s32[4,32]{1,0:T(4,128)...) while((s32[]{:T(128)}, f32[24,8192]{1,0:T(8,128)S(1)}, ...), condition=%wide.region_9.11_spmd, body=%wide.region_3.10_spmd.sunk | while | flops 679871104 | bytes 52703944 | solution.py:110
  52.2 1.7 %convolution_bitcast_fusion.5 = f32[2,1024,128]{2,1,0:T(8,128)} fusion(bf16[1,2,64,4,128]{4,3,2,1,0:T(4,128)(2,1)S(1)} %get-tuple-element.196, f32[2,4,64,1024]{3,2,1,0:T(8,128)S(1)} %get-tuple-element.194, f32[2,4,64]{2,1,0:T(4,128)S(1)} %get-tuple-element.195), kind=kOutput, calls=%fused_computation.16.clone.1 | convolution fusion | flops 135266304 | bytes 3278848 | tf_op jit(solution)/shard_map/while/body/eval_jaxpr/qgis,qigw->qsw/dot_general | solution.py:102
  55.3 2.1 %scatter_fusion.1 = f32[24,8192]{1,0:T(8,128)S(1)} fusion(f32[24,8192]{1,0:T(8,128)S(1)} %get-tuple-element.212, s32[32]{0:T(128)S(1)} %fusion.73, f32[32,8192]{1,0:T(8,128)S(1)} %reshape.340), kind=kCustom, calls=%fused_computation.3.clone.1 | custom fusion | flops 262144 | bytes 3145856 | tf_op jit(solution)/shard_map/while/body/eval_jaxpr/scatter-add | solution.py:106
  57.4 2.4 %fusion.76 = (f32[2,4,64]{2,1,0:T(4,128)S(1)}, f32[2,1024,64,4]{1,2,3,0:T(8,128)S(1)}) fusion(f32[2,4,64,1024]{3,2,1,0:T(8,128)} %copy-done, f32[2,4,64]{2,1,0:T(4,128)S(1)} %get-tuple-element.195, bf16[1,2,64,4,128]{4,3,2,1,0:T(4,128)(2,1)S(1)} %get-tuple-element.196, bf16[4,2,1024,128]{3,2,1,0:T(8,128)(2,1)} %get-tuple-element.229, s32[]{:T(128)S(6)} %copy.84), kind=kOutput, calls=%fused_computation.7.clone.1 | convolution fusion | flops 135790080 | bytes 4853764 | tf_op jit(solution)/shard_map/while/body/eval_jaxpr/qigw,qsw->qgis/dot_general | solution.py:91
  64.7 2.1 %scatter_fusion = f32[24,8192]{1,0:T(8,128)S(1)} fusion(f32[24,8192]{1,0:T(8,128)S(1)} %get-tuple-element.211, s32[32]{0:T(128)S(1)} %fusion.73, f32[32,8192]{1,0:T(8,128)S(1)} %reshape.339), kind=kCustom, calls=%fused_computation.2.clone.1 | custom fusion | flops 262144 | bytes 3145856 | tf_op jit(solution)/shard_map/while/body/eval_jaxpr/scatter-add | solution.py:105
  73.2 1.7 %convolution_bitcast_fusion.5 = f32[2,1024,128]{2,1,0:T(8,128)} fusion(bf16[1,2,64,4,128]{4,3,2,1,0:T(4,128)(2,1)S(1)} %get-tuple-element.196, f32[2,4,64,1024]{3,2,1,0:T(8,128)S(1)} %get-tuple-element.194, f32[2,4,64]{2,1,0:T(4,128)S(1)} %get-tuple-element.195), kind=kOutput, calls=%fused_computation.16.clone.1 | convolution fusion | flops 135266304 | bytes 3278848 | tf_op jit(solution)/shard_map/while/body/eval_jaxpr/qgis,qigw->qsw/dot_general | solution.py:102
  76.3 2.1 %scatter_fusion.1 = f32[24,8192]{1,0:T(8,128)S(1)} fusion(f32[24,8192]{1,0:T(8,128)S(1)} %get-tuple-element.212, s32[32]{0:T(128)S(1)} %fusion.73, f32[32,8192]{1,0:T(8,128)S(1)} %reshape.340), kind=kCustom, calls=%fused_computation.3.clone.1 | custom fusion | flops 262144 | bytes 3145856 | tf_op jit(solution)/shard_map/while/body/eval_jaxpr/scatter-add | solution.py:106
  78.4 2.4 %fusion.76 = (f32[2,4,64]{2,1,0:T(4,128)S(1)}, f32[2,1024,64,4]{1,2,3,0:T(8,128)S(1)}) fusion(f32[2,4,64,1024]{3,2,1,0:T(8,128)} %copy-done, f32[2,4,64]{2,1,0:T(4,128)S(1)} %get-tuple-element.195, bf16[1,2,64,4,128]{4,3,2,1,0:T(4,128)(2,1)S(1)} %get-tuple-element.196, bf16[4,2,1024,128]{3,2,1,0:T(8,128)(2,1)} %get-tuple-element.229, s32[]{:T(128)S(6)} %copy.84), kind=kOutput, calls=%fused_computation.7.clone.1 | convolution fusion | flops 135790080 | bytes 4853764 | tf_op jit(solution)/shard_map/while/body/eval_jaxpr/qigw,qsw->qgis/dot_general | solution.py:91
  85.7 2.1 %scatter_fusion = f32[24,8192]{1,0:T(8,128)S(1)} fusion(f32[24,8192]{1,0:T(8,128)S(1)} %get-tuple-element.211, s32[32]{0:T(128)S(1)} %fusion.73, f32[32,8192]{1,0:T(8,128)S(1)} %reshape.339), kind=kCustom, calls=%fused_computation.2.clone.1 | custom fusion | flops 262144 | bytes 3145856 | tf_op jit(solution)/shard_map/while/body/eval_jaxpr/scatter-add | solution.py:105
  97.3 2.1 %scatter_fusion.1 = f32[24,8192]{1,0:T(8,128)S(1)} fusion(f32[24,8192]{1,0:T(8,128)S(1)} %get-tuple-element.212, s32[32]{0:T(128)S(1)} %fusion.73, f32[32,8192]{1,0:T(8,128)S(1)} %reshape.340), kind=kCustom, calls=%fused_computation.3.clone.1 | custom fusion | flops 262144 | bytes 3145856 | tf_op jit(solution)/shard_map/while/body/eval_jaxpr/scatter-add | solution.py:106
  99.4 2.4 %fusion.76 = (f32[2,4,64]{2,1,0:T(4,128)S(1)}, f32[2,1024,64,4]{1,2,3,0:T(8,128)S(1)}) fusion(f32[2,4,64,1024]{3,2,1,0:T(8,128)} %copy-done, f32[2,4,64]{2,1,0:T(4,128)S(1)} %get-tuple-element.195, bf16[1,2,64,4,128]{4,3,2,1,0:T(4,128)(2,1)S(1)} %get-tuple-element.196, bf16[4,2,1024,128]{3,2,1,0:T(8,128)(2,1)} %get-tuple-element.229, s32[]{:T(128)S(6)} %copy.84), kind=kOutput, calls=%fused_computation.7.clone.1 | convolution fusion | flops 135790080 | bytes 4853764 | tf_op jit(solution)/shard_map/while/body/eval_jaxpr/qigw,qsw->qgis/dot_general | solution.py:91
  106.7 2.1 %scatter_fusion = f32[24,8192]{1,0:T(8,128)S(1)} fusion(f32[24,8192]{1,0:T(8,128)S(1)} %get-tuple-element.211, s32[32]{0:T(128)S(1)} %fusion.73, f32[32,8192]{1,0:T(8,128)S(1)} %reshape.339), kind=kCustom, calls=%fused_computation.2.clone.1 | custom fusion | flops 262144 | bytes 3145856 | tf_op jit(solution)/shard_map/while/body/eval_jaxpr/scatter-add | solution.py:105
  118.3 2.1 %scatter_fusion.1 = f32[24,8192]{1,0:T(8,128)S(1)} fusion(f32[24,8192]{1,0:T(8,128)S(1)} %get-tuple-element.212, s32[32]{0:T(128)S(1)} %fusion.73, f32[32,8192]{1,0:T(8,128)S(1)} %reshape.340), kind=kCustom, calls=%fused_computation.3.clone.1 | custom fusion | flops 262144 | bytes 3145856 | tf_op jit(solution)/shard_map/while/body/eval_jaxpr/scatter-add | solution.py:106
  120.4 2.4 %fusion.76 = (f32[2,4,64]{2,1,0:T(4,128)S(1)}, f32[2,1024,64,4]{1,2,3,0:T(8,128)S(1)}) fusion(f32[2,4,64,1024]{3,2,1,0:T(8,128)} %copy-done, f32[2,4,64]{2,1,0:T(4,128)S(1)} %get-tuple-element.195, bf16[1,2,64,4,128]{4,3,2,1,0:T(4,128)(2,1)S(1)} %get-tuple-element.196, bf16[4,2,1024,128]{3,2,1,0:T(8,128)(2,1)} %get-tuple-element.229, s32[]{:T(128)S(6)} %copy.84), kind=kOutput, calls=%fused_computation.7.clone.1 | convolution fusion | flops 135790080 | bytes 4853764 | tf_op jit(solution)/shard_map/while/body/eval_jaxpr/qigw,qsw->qgis/dot_general | solution.py:91
  127.7 2.1 %scatter_fusion = f32[24,8192]{1,0:T(8,128)S(1)} fusion(f32[24,8192]{1,0:T(8,128)S(1)} %get-tuple-element.211, s32[32]{0:T(128)S(1)} %fusion.73, f32[32,8192]{1,0:T(8,128)S(1)} %reshape.339), kind=kCustom, calls=%fused_computation.2.clone.1 | custom fusion | flops 262144 | bytes 3145856 | tf_op jit(solution)/shard_map/while/body/eval_jaxpr/scatter-add | solution.py:105
  131.5 4.1 %all-to-all-start = ((f32[4,4,8192]{2,1,0:T(4,128)}), f32[4,4,8192]{2,1,0:T(4,128)S(1)}, u32[]{:S(2)}, u32[]{:S(2)}) async-start(f32[4,4,8192]{2,1,0:T(4,128)} %reshape.280), calls=%async_computation | async-start | bytes 1048576 | tf_op jit(solution)/shard_map/all_to_all | solution.py:122
  137.0 8.9 %all-to-all-done = f32[4,4,8192]{2,1,0:T(4,128)S(1)} async-done(((f32[4,4,8192]{2,1,0:T(4,128)}), f32[4,4,8192]{2,1,0:T(4,128)S(1)}, u32[]{:S(2)}, u32[]{:S(2)}) %all-to-all-start) | async-done | bytes 524320 | tf_op jit(solution)/shard_map/all_to_all | solution.py:122
  146.0 3.5 %all-to-all-start.1 = ((f32[4,4,8192]{2,1,0:T(4,128)}), f32[4,4,8192]{2,1,0:T(4,128)S(1)}, u32[]{:S(2)}, u32[]{:S(2)}) async-start(f32[4,4,8192]{2,1,0:T(4,128)} %reshape.282), calls=%async_computation.1 | async-start | bytes 1048576 | tf_op jit(solution)/shard_map/all_to_all | solution.py:123
  150.7 9.0 %all-to-all-done.1 = f32[4,4,8192]{2,1,0:T(4,128)S(1)} async-done(((f32[4,4,8192]{2,1,0:T(4,128)}), f32[4,4,8192]{2,1,0:T(4,128)S(1)}, u32[]{:S(2)}, u32[]{:S(2)}) %all-to-all-start.1) | async-done | bytes 524320 | tf_op jit(solution)/shard_map/all_to_all | solution.py:123
  160.6 4.8 %all-reduce.2 = (bf16[8,8192]{1,0:T(8,128)(2,1)S(1)}, bf16[8,8192]{1,0:T(8,128)(2,1)S(1)}) all-reduce(f32[8,8192]{1,0:T(8,128)S(1)} %fusion.30, f32[8,8192]{1,0:T(8,128)S(1)} %fusion.31), channel_id=1, replica_groups=mesh['groups'=2,'seq'=4,'head'=2,'inner'=2] {'inner'}, use_global_device_ids=true, to_apply=%region_12.14 | all-reduce | flops 131072 | bytes 786432 | tf_op jit(solution)/shard_map/psum | solution.py:131
  (117 shorter events, 65.5 us)
Async XLA Ops:
  50.9 1.3 copy-start
  57.4 2.4 %copy-start.1 = (f32[2,4,64,1024]{3,2,1,0:T(8,128)S(1)}, f32[2,4,64,1024]{3,2,1,0:T(8,128)}, u32[]{:S(2)}) copy-start(f32[2,4,64,1024]{3,2,1,0:T(8,128)} %copy-done) | copy-start | bytes 6291460 | tf_op jit(solution)/shard_map/while
  71.9 1.3 copy-start
  78.4 2.4 %copy-start.1 = (f32[2,4,64,1024]{3,2,1,0:T(8,128)S(1)}, f32[2,4,64,1024]{3,2,1,0:T(8,128)}, u32[]{:S(2)}) copy-start(f32[2,4,64,1024]{3,2,1,0:T(8,128)} %copy-done) | copy-start | bytes 6291460 | tf_op jit(solution)/shard_map/while
  92.9 1.3 copy-start
  99.4 2.4 %copy-start.1 = (f32[2,4,64,1024]{3,2,1,0:T(8,128)S(1)}, f32[2,4,64,1024]{3,2,1,0:T(8,128)}, u32[]{:S(2)}) copy-start(f32[2,4,64,1024]{3,2,1,0:T(8,128)} %copy-done) | copy-start | bytes 6291460 | tf_op jit(solution)/shard_map/while
  113.9 1.3 copy-start
  120.4 2.4 %copy-start.1 = (f32[2,4,64,1024]{3,2,1,0:T(8,128)S(1)}, f32[2,4,64,1024]{3,2,1,0:T(8,128)}, u32[]{:S(2)}) copy-start(f32[2,4,64,1024]{3,2,1,0:T(8,128)} %copy-done) | copy-start | bytes 6291460 | tf_op jit(solution)/shard_map/while
  131.5 14.4 %all-to-all-start = ((f32[4,4,8192]{2,1,0:T(4,128)}), f32[4,4,8192]{2,1,0:T(4,128)S(1)}, u32[]{:S(2)}, u32[]{:S(2)}) async-start(f32[4,4,8192]{2,1,0:T(4,128)} %reshape.280), calls=%async_computation | async-start | bytes 1048576 | tf_op jit(solution)/shard_map/all_to_all | solution.py:122
  146.0 13.7 %all-to-all-start.1 = ((f32[4,4,8192]{2,1,0:T(4,128)}), f32[4,4,8192]{2,1,0:T(4,128)S(1)}, u32[]{:S(2)}, u32[]{:S(2)}) async-start(f32[4,4,8192]{2,1,0:T(4,128)} %reshape.282), calls=%async_computation.1 | async-start | bytes 1048576 | tf_op jit(solution)/shard_map/all_to_all | solution.py:123
where the time goes:
time: 168 us; the launch traced here: 167 us
  blocking collectives  39 us (23%)
  local copies, waits for them, and re-layouts  37.2 us (22%)
  matrix products  36.2 us (22%)
  other arithmetic  27.9 us (17%)
  waiting for transfers between devices  17.9 us (11%)
  starting transfers between devices  7.61 us (5%)
    all_gather x1, blocking collectives, per_device(): key_piece = lax.all_gather(keys, 'seq', axis=0, tiled=True)  17.6 us
    all_gather x1, blocking collectives, per_device(): value_piece = lax.all_gather(values, 'seq', axis=0, tiled=True)  16.6 us
    dot_general x4, matrix products, attend(): jnp.einsum('qigw,qsw->qgis', do_group, v_group, preferred_element_type=jn...  9.67 us
    all_to_all x1, waiting for transfers between devices, per_device(): lax.all_to_all(send_value_tiles, 'seq', split_axis=0, concat_axis=0, tile...  9 us
    all_to_all x1, waiting for transfers between devices, per_device(): lax.all_to_all(send_key_tiles, 'seq', split_axis=0, concat_axis=0, tiled=...  8.93 us
    scatter-add x4, other arithmetic, attend(): key_acc.at[rows_group].add(key_terms.reshape(group * TOPK, BLK * width))  8.42 us
    scatter-add x4, other arithmetic, attend(): value_acc.at[rows_group].add(value_terms.reshape(group * TOPK, BLK * width))  8.42 us
    dot_general x4, matrix products, attend(): jnp.einsum('qgis,qigw->qsw', probs_b, do_group, preferred_element_type=jn...  6.69 us
  transfers between devices with their start and end apart: 2, of which 2 were waited for; matrix products, arithmetic and copies ran while one was open for 2% of the time, Pallas kernels for 0%

commit v1 on v0

--- a/solution.py
+++ b/solution.py
@@ -48,8 +48,11 @@
     wanted = my_picks.reshape(-1)
     blank = jnp.zeros((blocks_here * TOPK, BLK, width), jnp.bfloat16)
     carry = (blank, blank)
-    key_piece = lax.all_gather(keys, "seq", axis=0, tiled=True)
-    value_piece = lax.all_gather(values, "seq", axis=0, tiled=True)
+    key_piece, value_piece = jnp.split(
+        lax.all_gather(jnp.concatenate([keys, values], axis=1), "seq", axis=0, tiled=True),
+        [keys.shape[1]],
+        axis=1,
+    )
     count = key_piece.shape[0] // BLK
     relative = wanted
     inside = (relative >= 0) & (relative < count)

time: 168 us -> 182 us (1.083)
  waiting for transfers between devices: 17.9 us -> 52.9 us
  blocking collectives: 39 us -> 4.84 us
  between operations: 0.82 us -> 14.2 us
    all_gather x2 -> x0, blocking collectives: 34.1 us -> none  [the longest x1 17.6 us: per_device(): key_piece = lax.all_gather(keys, 'seq', axis=0, tiled=True)]
    all_gather x0 -> x1, waiting for transfers between devices: none -> 27.2 us  [per_device(): lax.all_gather(jnp.concatenate([keys, values], axis=1), 'seq', axis=0, ti...]
    all_to_all x1, waiting for transfers between devices: 8.93 us -> 12.9 us  [per_device(): lax.all_to_all(send_key_tiles, 'seq', split_axis=0, concat_axis=0, tiled=...]
    all_to_all x1, waiting for transfers between devices: 9 us -> 12.8 us  [per_device(): lax.all_to_all(send_value_tiles, 'seq', split_axis=0, concat_axis=0, tile...]
    broadcast_in_dim x4, local copies, waits for them, and re-layouts: 3.66 us -> 0.05 us  [attend(): weights = jnp.where(mask_heads, jnp.exp(scores - highest), 0.0)]
  transfers between devices with their start and end apart: 2 -> 3, of which waited for: 2 -> 3; matrix products, arithmetic and copies ran while one was open for 2% -> 4% of each run, Pallas kernels for 0% -> 0%
where the time goes in v1:
time: 182 us; the launch traced here: 181 us
  waiting for transfers between devices  52.9 us (29%)
  matrix products  36.2 us (20%)
  local copies, waits for them, and re-layouts  36 us (20%)
  other arithmetic  29.1 us (16%)
  between operations  14.2 us (8%)
  starting transfers between devices  6.98 us (4%)
  blocking collectives  4.84 us (3%)
    all_gather x1, waiting for transfers between devices, per_device(): lax.all_gather(jnp.concatenate([keys, values], axis=1), 'seq', axis=0, ti...  27.2 us
    all_to_all x1, waiting for transfers between devices, per_device(): lax.all_to_all(send_key_tiles, 'seq', split_axis=0, concat_axis=0, tiled=...  12.9 us
    all_to_all x1, waiting for transfers between devices, per_device(): lax.all_to_all(send_value_tiles, 'seq', split_axis=0, concat_axis=0, tile...  12.8 us
    dot_general x4, matrix products, attend(): jnp.einsum('qigw,qsw->qgis', do_group, v_group, preferred_element_type=jn...  9.67 us
    scatter-add x4, other arithmetic, attend(): value_acc.at[rows_group].add(value_terms.reshape(group * TOPK, BLK * width))  8.42 us
    scatter-add x4, other arithmetic, attend(): key_acc.at[rows_group].add(key_terms.reshape(group * TOPK, BLK * width))  8.42 us
    dot_general x4, matrix products, attend(): jnp.einsum('qgis,qigw->qsw', probs_b, do_group, preferred_element_type=jn...  6.69 us
    dot_general x4, matrix products, attend(): jnp.einsum('qgis,qigw->qsw', dscores, q_group, preferred_element_type=jnp...  6.19 us
  transfers between devices with their start and end apart: 3, of which 3 were waited for; matrix products, arithmetic and copies ran while one was open for 4% of the time, Pallas kernels for 0%

profile of v1, /device:TPU:0, one launch (start us, length us, event | category | flops | bytes accessed | tf_op | source)
XLA Modules:
  0.0 180.6 jit_solution(9044020280022970847)
XLA Ops:
  7.2 1.7 pad_maximum_fusion
  13.1 27.2 %all-gather.2.cloned.1.call-done = bf16[2048,2,128]{2,0,1:T(8,128)(2,1)} async-done(((bf16[512,2,128]{2,0,1:T(8,128)(2,1)}), bf16[2048,2,128]{2,0,1:T(8,128)(2,1)}) %all-gather.2.cloned.1.call-update) | async-done | bytes 1048592 | tf_op jit(solution)/shard_map/all_gather | solution.py:52
  41.6 2.2 %gather_fusion = bf16[128,64,128]{2,1,0:T(8,128)(2,1)} fusion(bf16[32,64,128]{2,1,0:T(8,128)(2,1)S(1)} %bitcast.132, s32[1024]{0:T(1024)S(1)} %pad_clamp_fusion), kind=kCustom, calls=%fused_computation.clone | custom fusion | bytes 4194816 | tf_op jit(solution)/shard_map/jit(_take)/gather | solution.py:60
  43.7 2.1 %gather_fusion.1 = bf16[128,64,128]{2,1,0:T(8,128)(2,1)} fusion(bf16[32,64,128]{2,1,0:T(8,128)(2,1)S(1)} %bitcast.131, s32[1024]{0:T(1024)S(1)} %pad_clamp_fusion), kind=kCustom, calls=%fused_computation.1.clone | custom fusion | bytes 4194816 | tf_op jit(solution)/shard_map/jit(_take)/gather | solution.py:61
  45.9 4.0 %select_select_fusion = (bf16[128,64,128]{2,1,0:T(8,128)(2,1)}, bf16[128,64,128]{2,1,0:T(8,128)(2,1)}) fusion(bf16[128,64,128]{2,1,0:T(8,128)(2,1)} %gather_fusion.1, pred[128]{0:T(512)(128)(4,1)S(1)} %compare_and_fusion.2, pred[128]{0:T(512)(128)(4,1)S(1)} %and.166, bf16[128,64,128]{2,1,0:T(8,128)(2,1)} %gather_fusion), kind=kLoop, calls=%fused_computation.54 | loop fusion | flops 4194304 | bytes 8388864 | tf_op jit(solution)/shard_map/jit(_where)/select_n | solution.py:63
  50.0 80.4 %while.14 = (s32[]{:T(128)}, f32[24,8192]{1,0:T(8,128)S(1)}, f32[24,8192]{1,0:T(8,128)S(1)}, bf16[4,2,64,4,128]{4,3,2,1,0:T(4,128)(2,1)}, s32[4,32]{1,0:T(4,128)...) while((s32[]{:T(128)}, f32[24,8192]{1,0:T(8,128)S(1)}, ...), condition=%wide.region_9.11_spmd, body=%wide.region_3.10_spmd.sunk | while | flops 679871104 | bytes 52703944 | solution.py:113
  54.8 1.7 convolution_bitcast_fusion.5
  57.9 2.1 %scatter_fusion.1 = f32[24,8192]{1,0:T(8,128)S(1)} fusion(f32[24,8192]{1,0:T(8,128)S(1)} %get-tuple-element.214, s32[32]{0:T(128)S(1)} %fusion.74, f32[32,8192]{1,0:T(8,128)S(1)} %reshape.340), kind=kCustom, calls=%fused_computation.3.clone.1 | custom fusion | flops 262144 | bytes 3145856 | tf_op jit(solution)/shard_map/while/body/eval_jaxpr/scatter-add | solution.py:109
  60.0 2.4 %fusion.77 = (f32[2,4,64]{2,1,0:T(4,128)S(1)}, f32[2,1024,64,4]{1,2,3,0:T(8,128)S(1)}) fusion(f32[2,4,64,1024]{3,2,1,0:T(8,128)} %copy-done, f32[2,4,64]{2,1,0:T(4,128)S(1)} %get-tuple-element.197, bf16[1,2,64,4,128]{4,3,2,1,0:T(4,128)(2,1)S(1)} %get-tuple-element.198, bf16[4,2,1024,128]{3,2,1,0:T(8,128)(2,1)} %get-tuple-element.231, s32[]{:T(128)S(6)} %copy.84), kind=kOutput, calls=%fused_computation.7.clone.1 | convolution fusion | flops 135790080 | bytes 4853764 | tf_op jit(solution)/shard_map/while/body/eval_jaxpr/qigw,qsw->qgis/dot_general | solution.py:94
  67.2 2.1 %scatter_fusion = f32[24,8192]{1,0:T(8,128)S(1)} fusion(f32[24,8192]{1,0:T(8,128)S(1)} %get-tuple-element.213, s32[32]{0:T(128)S(1)} %fusion.74, f32[32,8192]{1,0:T(8,128)S(1)} %reshape.339), kind=kCustom, calls=%fused_computation.2.clone.1 | custom fusion | flops 262144 | bytes 3145856 | tf_op jit(solution)/shard_map/while/body/eval_jaxpr/scatter-add | solution.py:108
  77.9 2.1 %scatter_fusion.1 = f32[24,8192]{1,0:T(8,128)S(1)} fusion(f32[24,8192]{1,0:T(8,128)S(1)} %get-tuple-element.214, s32[32]{0:T(128)S(1)} %fusion.74, f32[32,8192]{1,0:T(8,128)S(1)} %reshape.340), kind=kCustom, calls=%fused_computation.3.clone.1 | custom fusion | flops 262144 | bytes 3145856 | tf_op jit(solution)/shard_map/while/body/eval_jaxpr/scatter-add | solution.py:109
  80.1 2.4 %fusion.77 = (f32[2,4,64]{2,1,0:T(4,128)S(1)}, f32[2,1024,64,4]{1,2,3,0:T(8,128)S(1)}) fusion(f32[2,4,64,1024]{3,2,1,0:T(8,128)} %copy-done, f32[2,4,64]{2,1,0:T(4,128)S(1)} %get-tuple-element.197, bf16[1,2,64,4,128]{4,3,2,1,0:T(4,128)(2,1)S(1)} %get-tuple-element.198, bf16[4,2,1024,128]{3,2,1,0:T(8,128)(2,1)} %get-tuple-element.231, s32[]{:T(128)S(6)} %copy.84), kind=kOutput, calls=%fused_computation.7.clone.1 | convolution fusion | flops 135790080 | bytes 4853764 | tf_op jit(solution)/shard_map/while/body/eval_jaxpr/qigw,qsw->qgis/dot_general | solution.py:94
  87.3 2.1 %scatter_fusion = f32[24,8192]{1,0:T(8,128)S(1)} fusion(f32[24,8192]{1,0:T(8,128)S(1)} %get-tuple-element.213, s32[32]{0:T(128)S(1)} %fusion.74, f32[32,8192]{1,0:T(8,128)S(1)} %reshape.339), kind=kCustom, calls=%fused_computation.2.clone.1 | custom fusion | flops 262144 | bytes 3145856 | tf_op jit(solution)/shard_map/while/body/eval_jaxpr/scatter-add | solution.py:108
  98.0 2.1 %scatter_fusion.1 = f32[24,8192]{1,0:T(8,128)S(1)} fusion(f32[24,8192]{1,0:T(8,128)S(1)} %get-tuple-element.214, s32[32]{0:T(128)S(1)} %fusion.74, f32[32,8192]{1,0:T(8,128)S(1)} %reshape.340), kind=kCustom, calls=%fused_computation.3.clone.1 | custom fusion | flops 262144 | bytes 3145856 | tf_op jit(solution)/shard_map/while/body/eval_jaxpr/scatter-add | solution.py:109
  100.2 2.4 %fusion.77 = (f32[2,4,64]{2,1,0:T(4,128)S(1)}, f32[2,1024,64,4]{1,2,3,0:T(8,128)S(1)}) fusion(f32[2,4,64,1024]{3,2,1,0:T(8,128)} %copy-done, f32[2,4,64]{2,1,0:T(4,128)S(1)} %get-tuple-element.197, bf16[1,2,64,4,128]{4,3,2,1,0:T(4,128)(2,1)S(1)} %get-tuple-element.198, bf16[4,2,1024,128]{3,2,1,0:T(8,128)(2,1)} %get-tuple-element.231, s32[]{:T(128)S(6)} %copy.84), kind=kOutput, calls=%fused_computation.7.clone.1 | convolution fusion | flops 135790080 | bytes 4853764 | tf_op jit(solution)/shard_map/while/body/eval_jaxpr/qigw,qsw->qgis/dot_general | solution.py:94
  107.4 2.1 %scatter_fusion = f32[24,8192]{1,0:T(8,128)S(1)} fusion(f32[24,8192]{1,0:T(8,128)S(1)} %get-tuple-element.213, s32[32]{0:T(128)S(1)} %fusion.74, f32[32,8192]{1,0:T(8,128)S(1)} %reshape.339), kind=kCustom, calls=%fused_computation.2.clone.1 | custom fusion | flops 262144 | bytes 3145856 | tf_op jit(solution)/shard_map/while/body/eval_jaxpr/scatter-add | solution.py:108
  118.1 2.1 %scatter_fusion.1 = f32[24,8192]{1,0:T(8,128)S(1)} fusion(f32[24,8192]{1,0:T(8,128)S(1)} %get-tuple-element.214, s32[32]{0:T(128)S(1)} %fusion.74, f32[32,8192]{1,0:T(8,128)S(1)} %reshape.340), kind=kCustom, calls=%fused_computation.3.clone.1 | custom fusion | flops 262144 | bytes 3145856 | tf_op jit(solution)/shard_map/while/body/eval_jaxpr/scatter-add | solution.py:109
  120.3 2.4 %fusion.77 = (f32[2,4,64]{2,1,0:T(4,128)S(1)}, f32[2,1024,64,4]{1,2,3,0:T(8,128)S(1)}) fusion(f32[2,4,64,1024]{3,2,1,0:T(8,128)} %copy-done, f32[2,4,64]{2,1,0:T(4,128)S(1)} %get-tuple-element.197, bf16[1,2,64,4,128]{4,3,2,1,0:T(4,128)(2,1)S(1)} %get-tuple-element.198, bf16[4,2,1024,128]{3,2,1,0:T(8,128)(2,1)} %get-tuple-element.231, s32[]{:T(128)S(6)} %copy.84), kind=kOutput, calls=%fused_computation.7.clone.1 | convolution fusion | flops 135790080 | bytes 4853764 | tf_op jit(solution)/shard_map/while/body/eval_jaxpr/qigw,qsw->qgis/dot_general | solution.py:94
  127.5 2.1 %scatter_fusion = f32[24,8192]{1,0:T(8,128)S(1)} fusion(f32[24,8192]{1,0:T(8,128)S(1)} %get-tuple-element.213, s32[32]{0:T(128)S(1)} %fusion.74, f32[32,8192]{1,0:T(8,128)S(1)} %reshape.339), kind=kCustom, calls=%fused_computation.2.clone.1 | custom fusion | flops 262144 | bytes 3145856 | tf_op jit(solution)/shard_map/while/body/eval_jaxpr/scatter-add | solution.py:108
  131.4 3.5 %all-to-all-start = ((f32[4,4,8192]{2,1,0:T(4,128)}), f32[4,4,8192]{2,1,0:T(4,128)S(1)}, u32[]{:S(2)}, u32[]{:S(2)}) async-start(f32[4,4,8192]{2,1,0:T(4,128)} %reshape.280), calls=%async_computation | async-start | bytes 1048576 | tf_op jit(solution)/shard_map/all_to_all | solution.py:125
  136.2 12.9 %all-to-all-done = f32[4,4,8192]{2,1,0:T(4,128)S(1)} async-done(((f32[4,4,8192]{2,1,0:T(4,128)}), f32[4,4,8192]{2,1,0:T(4,128)S(1)}, u32[]{:S(2)}, u32[]{:S(2)}) %all-to-all-start) | async-done | bytes 524320 | tf_op jit(solution)/shard_map/all_to_all | solution.py:125
  149.1 3.5 %all-to-all-start.1 = ((f32[4,4,8192]{2,1,0:T(4,128)}), f32[4,4,8192]{2,1,0:T(4,128)S(1)}, u32[]{:S(2)}, u32[]{:S(2)}) async-start(f32[4,4,8192]{2,1,0:T(4,128)} %reshape.282), calls=%async_computation.1 | async-start | bytes 1048576 | tf_op jit(solution)/shard_map/all_to_all | solution.py:126
  153.8 12.8 %all-to-all-done.1 = f32[4,4,8192]{2,1,0:T(4,128)S(1)} async-done(((f32[4,4,8192]{2,1,0:T(4,128)}), f32[4,4,8192]{2,1,0:T(4,128)S(1)}, u32[]{:S(2)}, u32[]{:S(2)}) %all-to-all-start.1) | async-done | bytes 524320 | tf_op jit(solution)/shard_map/all_to_all | solution.py:126
  167.5 4.8 %all-reduce.2 = (bf16[8,8192]{1,0:T(8,128)(2,1)S(1)}, bf16[8,8192]{1,0:T(8,128)(2,1)S(1)}) all-reduce(f32[8,8192]{1,0:T(8,128)S(1)} %fusion.30, f32[8,8192]{1,0:T(8,128)S(1)} %fusion.31), channel_id=1, replica_groups=mesh['groups'=2,'seq'=4,'head'=2,'inner'=2] {'inner'}, use_global_device_ids=true, to_apply=%region_12.14 | all-reduce | flops 131072 | bytes 786432 | tf_op jit(solution)/shard_map/psum | solution.py:134
  (120 shorter events, 63.2 us)
Async XLA Ops:
  7.2 33.1 %all-gather.2.cloned.1.call-start = ((), (), s32[]{:S(2)}) async-start(), calls=%async_computation.2 | async-start | bytes 1310720 | tf_op jit(solution)/shard_map/all_gather | solution.py:52
  53.5 1.3 copy-start
  60.0 2.4 %copy-start.1 = (f32[2,4,64,1024]{3,2,1,0:T(8,128)S(1)}, f32[2,4,64,1024]{3,2,1,0:T(8,128)}, u32[]{:S(2)}) copy-start(f32[2,4,64,1024]{3,2,1,0:T(8,128)} %copy-done) | copy-start | bytes 6291460 | tf_op jit(solution)/shard_map/while
  73.6 1.3 copy-start
  80.1 2.4 %copy-start.1 = (f32[2,4,64,1024]{3,2,1,0:T(8,128)S(1)}, f32[2,4,64,1024]{3,2,1,0:T(8,128)}, u32[]{:S(2)}) copy-start(f32[2,4,64,1024]{3,2,1,0:T(8,128)} %copy-done) | copy-start | bytes 6291460 | tf_op jit(solution)/shard_map/while
  93.7 1.3 copy-start
  100.2 2.4 %copy-start.1 = (f32[2,4,64,1024]{3,2,1,0:T(8,128)S(1)}, f32[2,4,64,1024]{3,2,1,0:T(8,128)}, u32[]{:S(2)}) copy-start(f32[2,4,64,1024]{3,2,1,0:T(8,128)} %copy-done) | copy-start | bytes 6291460 | tf_op jit(solution)/shard_map/while
  113.7 1.3 copy-start
  120.2 2.4 %copy-start.1 = (f32[2,4,64,1024]{3,2,1,0:T(8,128)S(1)}, f32[2,4,64,1024]{3,2,1,0:T(8,128)}, u32[]{:S(2)}) copy-start(f32[2,4,64,1024]{3,2,1,0:T(8,128)} %copy-done) | copy-start | bytes 6291460 | tf_op jit(solution)/shard_map/while
  131.4 17.7 %all-to-all-start = ((f32[4,4,8192]{2,1,0:T(4,128)}), f32[4,4,8192]{2,1,0:T(4,128)S(1)}, u32[]{:S(2)}, u32[]{:S(2)}) async-start(f32[4,4,8192]{2,1,0:T(4,128)} %reshape.280), calls=%async_computation | async-start | bytes 1048576 | tf_op jit(solution)/shard_map/all_to_all | solution.py:125
  149.1 17.5 %all-to-all-start.1 = ((f32[4,4,8192]{2,1,0:T(4,128)}), f32[4,4,8192]{2,1,0:T(4,128)S(1)}, u32[]{:S(2)}, u32[]{:S(2)}) async-start(f32[4,4,8192]{2,1,0:T(4,128)} %reshape.282), calls=%async_computation.1 | async-start | bytes 1048576 | tf_op jit(solution)/shard_map/all_to_all | solution.py:126
Sparse Core Ops, SparseCore 0:
  9.5 30.6 all-gather.1
